TPU v7x, 512 devices: a whole 4x8x8 slice. The times are simulated.
512 devices in a mesh: seed: 2 (over core), dp: 4 (over x), tensor: 64 (over z, y).
Axes of the slice: x: 4, y: 8, z: 8, core: 2. Of those that a mesh axis runs over, the one named last changes fastest.
Arguments:
- hidden: bfloat16 [2, 64, 96, 2048], P('seed', 'dp', None, 'tensor'), may hold values from -24 to 24
- norm_gain: float32 [2, 2048], P('seed'), may hold values from 0.25 to 1.75
- lm_head: bfloat16 [2, 2048, 65536], P('seed', None, 'tensor'), may hold values from -3 to 3
- targets: int32 [64, 96], P('dp'), may hold values from 0 to 65535
- lengths: int32 [64], P('dp'), may hold values from 24 to 96
Outputs:
- token_scores: float32 [2, 64, 96], P('seed', 'dp')
- ensemble: float32 [64], P('dp')
- centered: float32 [64], P('dp')
All inputs are finite; a program needn't handle non-finite values.
Results may differ from a plain program's by a relative error of at most 0.0003.
The roundings to bfloat16 on the way count: a program that leaves them out, or rounds other values in their place, can miss the bound.
Values may be sent and summed in bfloat16 or wider, within the bound.
A program may use at most 128 MiB of HBM per device.

v0:
```python
import jax
import jax.numpy as jnp
from jax import lax
from jax.sharding import Mesh
from jax.sharding import PartitionSpec as P

TENSOR = ("tensor_0", "tensor_1")
rms_epsilon = 1e-05


def gathered_once(x, axis):
    leaves = jax.tree.leaves(x)
    sequence = sorted(range(len(leaves)), key=lambda k: -leaves[k].size)
    width = (1, *leaves[sequence[0]].shape)[-1]
    lines = [
        jnp.pad(leaves[k].reshape(-1), (0, -leaves[k].size % width)).reshape(-1, width)
        for k in sequence
    ]
    both, at, found = (lax.all_gather(jnp.concatenate(lines), axis), 0, {})
    for k, line in zip(sequence, lines):
        piece = both[:, at : at + len(line)].reshape(len(both), -1)
        found[k] = piece[:, : leaves[k].size].reshape(-1, *leaves[k].shape)
        at += len(line)
    numbers = iter(range(len(leaves)))
    return jax.tree.map(lambda _: found[next(numbers)], x)


def joined_all(x, axes, combine):
    for axis in axes:
        pieces = gathered_once(x, axis)
        x = jax.tree.map(lambda part: part[0], pieces)
        for k in range(1, lax.axis_size(axis)):
            x = combine(x, jax.tree.map(lambda part: part[k], pieces))
    return x


def from_everyone(x, axis):
    peers = lax.axis_size(axis)
    return lax.all_to_all(jnp.broadcast_to(x[None], (peers, *x.shape)), axis, 0, 0, tiled=True)


def taken_together(x, axis):
    return from_everyone(x, axis).sum(axis=0)


def combine_parts(first, second):
    top_value = jnp.maximum(first[0], second[0])
    left = jnp.exp(first[0] - top_value)
    right = jnp.exp(second[0] - top_value)
    return (
        top_value,
        first[1] * left + second[1] * right,
        first[2] * left * left + second[2] * right * right,
        first[3] * left + second[3] * right,
    )


def shards(hidden, norm_gain, lm_head, targets, lengths):
    per_group, seq_len, own_width = (hidden.shape[1], hidden.shape[2], hidden.shape[3])
    full_width = norm_gain.shape[1]
    own_vocab = lm_head.shape[2]
    row_count = per_group * seq_len
    weight = lm_head[0]
    gain = norm_gain[0]
    whole = lax.all_gather(hidden, TENSOR, axis=3, tiled=True)
    flat = whole.reshape(row_count, full_width).astype(jnp.float32)
    mean_sq = jnp.mean(flat * flat, axis=1, keepdims=True)
    normed = (flat * lax.rsqrt(mean_sq + rms_epsilon) * gain).astype(jnp.bfloat16)
    logits = jnp.dot(normed, weight, preferred_element_type=jnp.float32)
    first_column = lax.axis_index(TENSOR) * own_vocab
    column = jnp.arange(own_vocab, dtype=jnp.int32) + first_column
    onehot = column[None, :] == targets.reshape(row_count)[:, None]
    local_top = jnp.max(logits, axis=1)
    scaled_exp = jnp.exp(logits - local_top[:, None])
    merged = joined_all(
        (
            local_top,
            jnp.sum(scaled_exp, axis=1),
            jnp.sum(scaled_exp * scaled_exp, axis=1),
            jnp.sum(jnp.where(onehot, scaled_exp, 0.0), axis=1),
        ),
        TENSOR,
        combine_parts,
    )
    exp_mass, exp_square, exp_target = (merged[1], merged[2], merged[3])
    spread = jnp.maximum(
        exp_square / (exp_mass * exp_mass) - 2.0 * exp_target / exp_mass + 1.0, 0.0
    )
    scores = jnp.sqrt(spread).reshape(per_group, seq_len)
    position = jnp.arange(seq_len, dtype=jnp.int32)
    valid = position[None, :] < lengths[:, None]
    token_scores = jnp.where(valid, scores, jnp.float32(0.0))
    example_scores = jnp.sum(token_scores, axis=1) / lengths.astype(jnp.float32)
    members = lax.axis_size("seed")
    groups = lax.axis_size("dp")
    slots = jnp.zeros((groups * per_group,), jnp.float32)
    slots = lax.dynamic_update_slice_in_dim(
        slots, example_scores, lax.axis_index("dp") * per_group, 0
    )
    everyone = taken_together(slots, ("seed", "dp")) / members
    ensemble = lax.dynamic_slice_in_dim(everyone, lax.axis_index("dp") * per_group, per_group, 0)
    centered = ensemble - jnp.sum(everyone) / (per_group * groups)
    return (token_scores[None, :, :], ensemble, centered)


def solution(mesh):
    finer = Mesh(
        mesh.devices.reshape(mesh.shape["seed"], mesh.shape["dp"], 8, 8),
        ("seed", "dp", "tensor_0", "tensor_1"),
    )
    in_specs = (
        P("seed", "dp", None, TENSOR),
        P("seed", None),
        P("seed", None, TENSOR),
        P("dp", None),
        P("dp"),
    )
    out_specs = (P("seed", "dp", None), P("dp"), P("dp"))
    return jax.shard_map(
        shards, mesh=finer, in_specs=in_specs, out_specs=out_specs, check_vma=False
    )
```

profile of v0, /device:TPU:1, one launch (start us, length us, event | category | flops | bytes accessed | tf_op | source)
XLA Modules:
  0.0 219.5 jit_solution(6617547372947440160)
XLA Ops:
  7.2 1.6 copy.13
  8.9 0.8 eq.16
  9.6 105.8 %all-gather.6.cloned.1.call-done = bf16[1,16,96,2048]{2,1,0,3:T(8,128)(2,1)} async-done(((bf16[1,16,96,32]{2,1,0,3:T(8,128)(2,1)}), bf16[1,16,96,2048]{2,1,0,3:T(8,128)(2,1)}) %all-gather.6.cloned.1.call-update) | async-done | bytes 6291472 | tf_op jit(solution)/shard_map/all_gather | solution.py:65
  115.4 11.8 %copy.14 = bf16[1,16,96,2048]{3,2,1,0:T(8,128)(2,1)} copy(bf16[1,16,96,2048]{2,1,0,3:T(8,128)(2,1)} %all-gather.6.cloned.1.call-done) | data formatting | bytes 12582912 | tf_op jit(solution)/shard_map/all_gather | solution.py:65
  127.2 4.2 %fusion = f32[16,96]{1,0:T(8,128)S(1)} fusion(bf16[1,16,96,2048]{3,2,1,0:T(8,128)(2,1)} %copy.14), kind=kLoop, calls=%fused_computation.2 | loop fusion | flops 9435648 | bytes 6297600 | tf_op jit(solution)/shard_map/reduce_sum | solution.py:67
  131.4 0.3 copy-done
  131.8 1.5 fusion.2
  133.3 0.7 copy-done.3
  134.0 7.4 %fusion.103 = (f32[1536]{0:T(1024)S(1)}, f32[1536,1024]{0,1:T(8,128)S(1)}) fusion(bf16[1536,2048]{1,0:T(8,128)(2,1)S(1)} %bitcast.341, bf16[1,2048,1024]{2,1,0:T(8,128)(2,1)S(1)} %copy-done.3), kind=kOutput, calls=%fused_computation.251 | convolution fusion | flops 6444022272 | bytes 16783360 | tf_op jit(solution)/shard_map/dot_general | solution.py:69
  141.4 2.3 %fusion.3 = (f32[1536]{0:T(1024)S(1)}, f32[1536]{0:T(1024)S(1)}, f32[1536]{0:T(1024)S(1)}) fusion(f32[1536,1024]{0,1:T(8,128)S(1)} %get-tuple-element.48, f32[1536]{0:T(1024)S(1)} %get-tuple-element.47, s32[1536]{0:T(1024)S(1)} %eq.16, s32[1024]{0:T(1024)S(1)} %iota_add_fusion), kind=kLoop, calls=%fused_computation.8 | loop fusion | flops 11005440 | bytes 6326272 | tf_op jit(solution)/shard_map/reduce_sum | solution.py:78
  143.8 19.5 %all-gather.2 = f32[8,4,1536]{2,1,0:T(4,128)S(1)} all-gather(f32[1,4,1536]{2,1,0:T(4,128)S(1)} %maximum_bitcast_fusion), channel_id=2, replica_groups=mesh['seed'=2,'dp'=4,'tensor_0'=8,'tensor_1'=8] {'tensor_0'}, dimensions={0}, use_global_device_ids=true | all-gather | bytes 221184 | tf_op jit(solution)/shard_map/all_gather | solution.py:19
  163.4 0.1 fusion.71
  163.5 0.2 fusion.48
  163.7 0.1 fusion.50
  163.9 18.9 %all-gather.3 = f32[8,4,1536]{2,1,0:T(4,128)S(1)} all-gather(f32[1,4,1536]{2,1,0:T(4,128)S(1)} %maximum_bitcast_fusion.1), channel_id=3, replica_groups=mesh['seed'=2,'dp'=4,'tensor_0'=8,'tensor_1'=8] {'tensor_1'}, dimensions={0}, use_global_device_ids=true | all-gather | bytes 221184 | tf_op jit(solution)/shard_map/all_gather | solution.py:19
  182.7 0.3 slice_reduce_fusion.30
  183.0 0.2 slice_reduce_fusion.31
  183.3 0.1 squeeze.325
  186.1 0.1 squeeze.326
  186.2 0.1 squeeze.294
  186.3 0.1 squeeze.327
  186.3 0.1 squeeze.295
  186.4 0.1 squeeze.328
  186.5 0.1 squeeze.296
  186.6 0.1 squeeze.297
  186.7 0.1 squeeze.330
  186.8 0.1 squeeze.298
  186.8 0.1 squeeze.331
  186.9 0.1 squeeze.299
  187.0 0.1 squeeze.332
  187.1 0.1 squeeze.300
  187.1 0.1 squeeze.333
  187.2 0.1 squeeze.301
  187.3 0.1 squeeze.334
  187.4 0.1 squeeze.302
  187.4 0.1 squeeze.335
  187.5 0.1 squeeze.303
  187.6 0.1 squeeze.336
  187.7 0.1 squeeze.304
  187.7 0.1 squeeze.355
  187.9 0.2 select_reduce_fusion.1
  188.1 0.1 divide_dynamic-update-slice_fusion
  188.2 0.6 broadcast_in_dim.8
  188.8 17.4 %all-to-all-start = ((f32[8,1,64]{2,1,0:T(1,128)}), f32[8,1,64]{2,1,0:T(1,128)S(1)}, u32[]{:S(2)}, u32[]{:S(2)}) async-start(f32[8,1,64]{2,1,0:T(1,128)} %broadcast_in_dim.8), calls=%async_computation | async-start | bytes 8192 | tf_op jit(solution)/shard_map/all_to_all | solution.py:39
  206.2 0.7 sqrt_select_fusion
  206.9 3.9 %all-to-all-done = f32[8,1,64]{2,1,0:T(1,128)S(1)} async-done(((f32[8,1,64]{2,1,0:T(1,128)}), f32[8,1,64]{2,1,0:T(1,128)S(1)}, u32[]{:S(2)}, u32[]{:S(2)}) %all-to-all-start) | async-done | bytes 2080 | tf_op jit(solution)/shard_map/all_to_all | solution.py:39
  210.8 0.6 broadcast_multiply_fusion
  212.1 0.6 broadcast_subtract_fusion
  (59 shorter events, 3.1 us)
Async XLA Ops:
  7.2 108.2 %all-gather.6.cloned.1.call-start = ((), (), s32[]{:S(2)}) async-start(), calls=%async_computation.1 | async-start | bytes 8519680 | tf_op jit(solution)/shard_map/all_gather | solution.py:65
  127.2 4.6 %copy-start = (bf16[1,16,96,2048]{3,2,1,0:T(8,128)(2,1)S(1)}, bf16[1,16,96,2048]{3,2,1,0:T(8,128)(2,1)}, u32[]{:S(2)}) copy-start(bf16[1,16,96,2048]{3,2,1,0:T(8,128)(2,1)} %copy.14) | copy-start | bytes 18874372
  127.2 4.6 %copy-start.1 = (f32[1,2048]{1,0:T(1,128)S(1)}, f32[1,2048]{1,0:T(1,128)}, u32[]{:S(2)}) copy-start(f32[1,2048]{1,0:T(1,128)} %param.6) | copy-start | bytes 24580
  131.8 2.2 copy-start.3
  141.4 46.5 %copy-start.2 = (s32[16]{0:T(128)S(1)}, s32[16]{0:T(128)}, u32[]{:S(2)}) copy-start(s32[16]{0:T(128)} %param.9) | copy-start | bytes 196
  188.8 22.0 %all-to-all-start = ((f32[8,1,64]{2,1,0:T(1,128)}), f32[8,1,64]{2,1,0:T(1,128)S(1)}, u32[]{:S(2)}, u32[]{:S(2)}) async-start(f32[8,1,64]{2,1,0:T(1,128)} %broadcast_in_dim.8), calls=%async_computation | async-start | bytes 8192 | tf_op jit(solution)/shard_map/all_to_all | solution.py:39
Sparse Core Ops, SparseCore 0:
  11.0 104.3 all-gather.5
where the time goes:
time: 220 us
  waiting for transfers between devices  110 us (50%)
  blocking collectives  38.4 us (17%)
  local copies, waits for them, and re-layouts  20.9 us (10%)
  starting transfers between devices  17.4 us (8%)
  between operations  14.9 us (7%)
  other arithmetic  10.9 us (5%)
  matrix products  7.38 us (3%)
    all_gather x1, waiting for transfers between devices, shards(): whole = lax.all_gather(hidden, TENSOR, axis=3, tiled=True)  106 us
    all_gather x2, blocking collectives, gathered_once(): both, at, found = (lax.all_gather(jnp.concatenate(lines), axis), 0, {})  38.4 us
    all_to_all x1, starting transfers between devices, from_everyone(): lax.all_to_all(jnp.broadcast_to(x[None], (peers, *x.shape)), axis, 0, 0,...  17.4 us
    all_gather x1, local copies, waits for them, and re-layouts, shards(): whole = lax.all_gather(hidden, TENSOR, axis=3, tiled=True)  11.8 us
    dot_general x1, matrix products, shards(): logits = jnp.dot(normed, weight, preferred_element_type=jnp.float32)  7.38 us
  transfers between devices with their start and end apart: 2, of which 2 were waited for; matrix products, arithmetic and copies ran while one was open for 1% of the time, Pallas kernels for 0%

commit v1 on v0

--- a/solution.py
+++ b/solution.py
@@ -62,7 +62,9 @@
     row_count = per_group * seq_len
     weight = lm_head[0]
     gain = norm_gain[0]
-    whole = lax.all_gather(hidden, TENSOR, axis=3, tiled=True)
+    whole = jnp.concatenate(
+        lax.all_to_all(jnp.stack([hidden] * lax.axis_size(TENSOR)), TENSOR, 0, 0), axis=3
+    )
     flat = whole.reshape(row_count, full_width).astype(jnp.float32)
     mean_sq = jnp.mean(flat * flat, axis=1, keepdims=True)
     normed = (flat * lax.rsqrt(mean_sq + rms_epsilon) * gain).astype(jnp.bfloat16)

time: 220 us -> 406 us (1.85)
  waiting for transfers between devices: 110 us -> 244 us
  blocking collectives: 38.4 us -> 67.3 us
  starting transfers between devices: 17.4 us -> 34.7 us
  between operations: 14.9 us -> 1.48 us
  other arithmetic: 10.9 us -> 19.3 us
  local copies, waits for them, and re-layouts: 20.9 us -> 27.1 us
    all_to_all x0 -> x1, waiting for transfers between devices: none -> 240 us  [shards(): lax.all_to_all(jnp.stack([hidden] * lax.axis_size(TENSOR)), TENSOR, 0, 0)]
    all_gather x1 -> x0, waiting for transfers between devices: 106 us -> none  [shards(): whole = lax.all_gather(hidden, TENSOR, axis=3, tiled=True)]
    all_gather x2, blocking collectives: 38.4 us -> 67.3 us  [gathered_once(): both, at, found = (lax.all_gather(jnp.concatenate(lines), axis), 0, {})]
    all_to_all x0 -> x1, starting transfers between devices: none -> 17.5 us  [shards(): lax.all_to_all(jnp.stack([hidden] * lax.axis_size(TENSOR)), TENSOR, 0, 0)]
    convert_element_type x0 -> x1, local copies, waits for them, and re-layouts: none -> 14.5 us  [shards(): (flat * lax.rsqrt(mean_sq + rms_epsilon) * gain).astype(jnp.bfloat16)]
    all_gather x1 -> x0, local copies, waits for them, and re-layouts: 11.8 us -> none  [shards(): whole = lax.all_gather(hidden, TENSOR, axis=3, tiled=True)]
    convert_element_type x1, other arithmetic: 1.53 us -> 7.94 us  [shards(): (flat * lax.rsqrt(mean_sq + rms_epsilon) * gain).astype(jnp.bfloat16)]
    another operation x0 -> x2, local copies, waits for them, and re-layouts: none -> 6.19 us  [the longest x1 5.23 us: shards(): jnp.stack([hidden] * lax.axis_size(TENSOR))]
  transfers between devices with their start and end apart: 2 -> 2, of which waited for: 2 -> 2; matrix products, arithmetic and copies ran while one was open for 1% -> 0% of each run, Pallas kernels for 0% -> 0%
where the time goes in v1:
time: 406 us; the launch traced here: 405 us
  waiting for transfers between devices  244 us (60%)
  blocking collectives  67.3 us (17%)
  starting transfers between devices  34.7 us (9%)
  local copies, waits for them, and re-layouts  27.1 us (7%)
  other arithmetic  19.3 us (5%)
  matrix products  10.6 us (3%)
    all_to_all x1, waiting for transfers between devices, shards(): lax.all_to_all(jnp.stack([hidden] * lax.axis_size(TENSOR)), TENSOR, 0, 0)  240 us
    all_gather x2, blocking collectives, gathered_once(): both, at, found = (lax.all_gather(jnp.concatenate(lines), axis), 0, {})  67.3 us
    all_to_all x1, starting transfers between devices, shards(): lax.all_to_all(jnp.stack([hidden] * lax.axis_size(TENSOR)), TENSOR, 0, 0)  17.5 us
    all_to_all x1, starting transfers between devices, from_everyone(): lax.all_to_all(jnp.broadcast_to(x[None], (peers, *x.shape)), axis, 0, 0,...  17.1 us
    convert_element_type x1, local copies, waits for them, and re-layouts, shards(): (flat * lax.rsqrt(mean_sq + rms_epsilon) * gain).astype(jnp.bfloat16)  14.5 us
    dot_general x1, matrix products, shards(): logits = jnp.dot(normed, weight, preferred_element_type=jnp.float32)  10.6 us
  transfers between devices with their start and end apart: 2, of which 2 were waited for; matrix products, arithmetic and copies ran while one was open for 0% of the time, Pallas kernels for 0%

profile of v1, /device:TPU:1, one launch (start us, length us, event | category | flops | bytes accessed | tf_op | source)
XLA Modules:
  0.0 404.9 jit_solution(5032539184284307139)
XLA Ops:
  0.6 1.0 copy.12
  1.6 5.2 %stack.2 = bf16[64,1,16,96,32]{3,2,4,1,0:T(8,128)(2,1)} broadcast(bf16[16,96,32]{1,0,2:T(8,128)(2,1)S(1)} %copy.12), dimensions={2,3,4} | broadcast | bytes 6389760 | tf_op jit(solution)/shard_map/stack | solution.py:66
  6.8 17.5 %all-to-all-start = ((bf16[64,1,16,96,32]{3,2,4,1,0:T(8,128)(2,1)}), bf16[64,1,16,96,32]{3,2,4,1,0:T(8,128)(2,1)}, u32[]{:S(2)}, u32[]{:S(2)}) async-start(bf16[64,1,16,96,32]{3,2,4,1,0:T(8,128)(2,1)} %stack.2), calls=%async_computation | async-start | bytes 16777216 | tf_op jit(solution)/shard_map/all_to_all | solution.py:66
  24.4 0.5 broadcast.191
  24.9 0.7 reduce.102
  25.6 0.1 eq.16
  25.7 240.5 %all-to-all-done = bf16[64,1,16,96,32]{3,2,4,1,0:T(8,128)(2,1)} async-done(((bf16[64,1,16,96,32]{3,2,4,1,0:T(8,128)(2,1)}), bf16[64,1,16,96,32]{3,2,4,1,0:T(8,128)(2,1)}, u32[]{:S(2)}, u32[]{:S(2)}) %all-to-all-start) | async-done | bytes 6291488 | tf_op jit(solution)/shard_map/all_to_all | solution.py:66
  266.2 5.6 %fusion = f32[16,96]{1,0:T(8,128)S(1)} fusion(bf16[64,1,16,96,32]{3,2,4,1,0:T(8,128)(2,1)} %all-to-all-done), kind=kLoop, calls=%fused_computation.2 | loop fusion | flops 9435648 | bytes 6297600 | tf_op jit(solution)/shard_map/reduce_sum | solution.py:69
  271.8 7.9 %fusion.3 = bf16[1,16,96,64,32]{2,1,4,0,3:T(8,128)(2,1)} fusion(bf16[64,1,16,96,32]{3,2,4,1,0:T(8,128)(2,1)} %all-to-all-done, f32[64,32]{1,0:T(8,128)S(1)} %mul.1594, f32[16,96]{1,0:T(8,128)S(1)} %add_rsqrt_fusion), kind=kLoop, calls=%fused_computation.5 | loop fusion | flops 12582912 | bytes 12597248 | tf_op jit(solution)/shard_map/convert_element_type | solution.py:70
  279.7 14.5 %convert_element_type.21 = bf16[1536,2048]{0,1:T(8,128)(2,1)} reshape(bf16[1,16,96,64,32]{2,1,4,0,3:T(8,128)(2,1)} %fusion.3) | data formatting | bytes 12582912 | tf_op jit(solution)/shard_map/convert_element_type | solution.py:70
  294.3 10.6 %fusion.104 = (f32[1536]{0:T(1024)S(1)}, f32[1536,1024]{0,1:T(8,128)S(1)}) fusion(bf16[1536,2048]{0,1:T(8,128)(2,1)} %convert_element_type.21, bf16[1,2048,1024]{2,1,0:T(8,128)(2,1)} %param.7), kind=kOutput, calls=%fused_computation.252 | convolution fusion | flops 6444022272 | bytes 16783360 | tf_op jit(solution)/shard_map/dot_general | solution.py:71
  304.9 2.3 fusion.4
  307.3 34.4 %all-gather.2 = f32[8,4,1536]{2,1,0:T(4,128)S(1)} all-gather(f32[1,4,1536]{2,1,0:T(4,128)S(1)} %maximum_bitcast_fusion), channel_id=2, replica_groups=mesh['seed'=2,'dp'=4,'tensor_0'=8,'tensor_1'=8] {'tensor_0'}, dimensions={0}, use_global_device_ids=true | all-gather | bytes 221184 | tf_op jit(solution)/shard_map/all_gather | solution.py:19
  341.8 0.1 fusion.72
  341.9 0.2 fusion.49
  342.1 0.1 fusion.51
  342.3 32.9 %all-gather.3 = f32[8,4,1536]{2,1,0:T(4,128)S(1)} all-gather(f32[1,4,1536]{2,1,0:T(4,128)S(1)} %maximum_bitcast_fusion.1), channel_id=3, replica_groups=mesh['seed'=2,'dp'=4,'tensor_0'=8,'tensor_1'=8] {'tensor_1'}, dimensions={0}, use_global_device_ids=true | all-gather | bytes 221184 | tf_op jit(solution)/shard_map/all_gather | solution.py:19
  375.2 0.3 slice_reduce_fusion.30
  375.5 0.2 slice_reduce_fusion.31
  375.7 0.1 squeeze.325
  378.7 0.1 squeeze.294
  378.7 0.1 squeeze.327
  378.8 0.1 squeeze.295
  378.9 0.1 squeeze.328
  378.9 0.1 squeeze.296
  379.0 0.1 squeeze.329
  379.1 0.1 squeeze.297
  379.2 0.1 squeeze.330
  379.2 0.1 squeeze.298
  379.3 0.1 squeeze.331
  379.4 0.1 squeeze.299
  379.5 0.1 squeeze.332
  379.5 0.1 squeeze.300
  379.6 0.1 squeeze.333
  379.7 0.1 squeeze.301
  379.7 0.1 squeeze.334
  379.8 0.1 squeeze.302
  379.9 0.1 squeeze.335
  380.0 0.1 squeeze.336
  380.1 0.1 squeeze.304
  380.3 0.2 select_reduce_fusion.1
  380.6 0.1 divide_dynamic-update-slice_fusion
  380.7 0.6 broadcast_in_dim.8
  381.3 17.1 %all-to-all-start.1 = ((f32[8,1,64]{2,1,0:T(1,128)}), f32[8,1,64]{2,1,0:T(1,128)S(1)}, u32[]{:S(2)}, u32[]{:S(2)}) async-start(f32[8,1,64]{2,1,0:T(1,128)} %broadcast_in_dim.8), calls=%async_computation.1 | async-start | bytes 8192 | tf_op jit(solution)/shard_map/all_to_all | solution.py:39
  398.4 0.7 sqrt_select_fusion
  399.1 3.9 all-to-all-done.1
  403.1 0.6 broadcast_multiply_fusion
  404.3 0.6 broadcast_subtract_fusion
  (60 shorter events, 3.3 us)
Async XLA Ops:
  6.8 18.1 %copy-start = (f32[1,2048]{1,0:T(1,128)S(1)}, f32[1,2048]{1,0:T(1,128)}, u32[]{:S(2)}) copy-start(f32[1,2048]{1,0:T(1,128)} %param.6) | copy-start | bytes 24580
  6.8 18.8 %copy-start.1 = (s32[16,96]{1,0:T(8,128)S(1)}, s32[16,96]{1,0:T(8,128)}, u32[]{:S(2)}) copy-start(s32[16,96]{1,0:T(8,128)} %param.8) | copy-start | bytes 18436
  6.8 259.3 %all-to-all-start = ((bf16[64,1,16,96,32]{3,2,4,1,0:T(8,128)(2,1)}), bf16[64,1,16,96,32]{3,2,4,1,0:T(8,128)(2,1)}, u32[]{:S(2)}, u32[]{:S(2)}) async-start(bf16[64,1,16,96,32]{3,2,4,1,0:T(8,128)(2,1)} %stack.2), calls=%async_computation | async-start | bytes 16777216 | tf_op jit(solution)/shard_map/all_to_all | solution.py:66
  304.9 75.5 %copy-start.2 = (s32[16]{0:T(128)S(1)}, s32[16]{0:T(128)}, u32[]{:S(2)}) copy-start(s32[16]{0:T(128)} %param.9) | copy-start | bytes 196
  381.3 21.7 %all-to-all-start.1 = ((f32[8,1,64]{2,1,0:T(1,128)}), f32[8,1,64]{2,1,0:T(1,128)S(1)}, u32[]{:S(2)}, u32[]{:S(2)}) async-start(f32[8,1,64]{2,1,0:T(1,128)} %broadcast_in_dim.8), calls=%async_computation.1 | async-start | bytes 8192 | tf_op jit(solution)/shard_map/all_to_all | solution.py:39
